TPU v7x, 32 devices: a whole 2x2x4 slice. The times are simulated.
32 devices in a mesh: corpus: 16 (over z, y, x), tensor: 2 (over core).
Axes of the slice: x: 2, y: 2, z: 4, core: 2. Of those that a mesh axis runs over, the one named last changes fastest.
Arguments:
- q_states: bfloat16 [1024, 4096], P('corpus', 'tensor'), may hold values from -90 to 90
- k_states: bfloat16 [1024, 1024], P('corpus', 'tensor'), may hold values from -9 to 9
- v_states: bfloat16 [1024, 1024], P('corpus', 'tensor'), may hold values from -6 to 6
- residual: bfloat16 [1024, 4096], P('corpus'), may hold values from -170 to 170
- out_weight: bfloat16 [4096, 4096], P('tensor'), may hold values from -0.09375 to 0.09375
- final_gain: float32 [4096], replicated, may hold values from 0.25 to 1.75
- passages: bfloat16 [8192, 4096], P(('corpus', 'tensor')), may hold values from -5 to 5
- lengths: int32 [64], P('corpus'), may hold values from 1 to 16
Outputs:
- scores: float32 [64, 8192], P(None, ('corpus', 'tensor'))
- log_norm: float32 [64], replicated
All inputs are finite; a program needn't handle non-finite values.
Results may differ from a plain program's by a relative error of at most 0.0003.
The roundings to bfloat16 on the way count: a program that leaves them out, or rounds other values in their place, can miss the bound.
Values may be sent and summed in bfloat16 or wider, within the bound.
A program may use at most 64 MiB of HBM per device.

v0:
```python
import math
import jax
import jax.numpy as jnp
from jax import lax
from jax.sharding import PartitionSpec as P

HEAD_DIM = 128
SEQ = 16
score_scale = 50.0


def merged(value, axis, join):
    pieces = jax.tree.map(lambda part: lax.all_gather(part, axis), value)
    head = jax.tree.map(lambda part: part[0], pieces)
    tail = jax.tree.map(lambda part: part[1:], pieces)
    total, _ = lax.scan(lambda total, piece: (join(total, piece), None), head, tail)
    return total


def attend_last(queries, key_rows, value_rows, lengths):
    query_count = queries.shape[0]
    pair_heads = key_rows.shape[2] // HEAD_DIM
    grouped = queries.reshape(query_count, pair_heads, -1, HEAD_DIM)
    keyed = key_rows.reshape(query_count, SEQ, pair_heads, HEAD_DIM)
    valued = value_rows.reshape(query_count, SEQ, pair_heads, HEAD_DIM)
    logits = jnp.einsum(
        "bkgd,bskd->bkgs", grouped, keyed, preferred_element_type=jnp.float32
    ) / math.sqrt(HEAD_DIM)
    key_place = lax.broadcasted_iota(jnp.int32, (1, SEQ), 1)
    allowed = (key_place < lengths[:, None])[:, None, None, :]
    logits = jnp.where(allowed, logits, -1e30)
    highest = jnp.max(logits, axis=-1, keepdims=True)
    weights = jnp.where(allowed, jnp.exp(logits - highest), 0.0)
    attention = (weights / jnp.sum(weights, axis=-1, keepdims=True)).astype(jnp.bfloat16)
    context = jnp.einsum("bkgs,bskd->bkgd", attention, valued, preferred_element_type=jnp.float32)
    return context.reshape(query_count, -1).astype(jnp.bfloat16)


def normalize_rows(pooled, final_gain):
    scaled = pooled * final_gain[None, :]
    magnitude = jnp.maximum(jnp.sqrt(jnp.sum(scaled * scaled, axis=1, keepdims=True)), 1.0)
    return (scaled / magnitude).astype(jnp.bfloat16)


def on_device(q_states, k_states, v_states, residual, out_weight, final_gain, passages, lengths):
    query_count = lengths.shape[0]
    places = lax.broadcasted_iota(jnp.int32, (query_count, SEQ), 1)
    picked = (places == (lengths - 1)[:, None])[:, :, None]
    key_rows = k_states.reshape(query_count, SEQ, -1)
    value_rows = v_states.reshape(query_count, SEQ, -1)
    last_query = jnp.sum(
        jnp.where(picked, q_states.reshape(query_count, SEQ, -1).astype(jnp.float32), 0.0), axis=1
    ).astype(jnp.bfloat16)
    last_residual = jnp.sum(
        jnp.where(picked, residual.reshape(query_count, SEQ, -1).astype(jnp.float32), 0.0), axis=1
    )
    context = attend_last(last_query, key_rows, value_rows, lengths)
    partial_value = jnp.dot(context, out_weight, preferred_element_type=jnp.float32)
    pooled = last_residual + lax.psum(partial_value, "tensor")
    embed = normalize_rows(pooled, final_gain)
    scores = (
        lax.dot_general(
            lax.all_gather(embed, "corpus", axis=0, tiled=True),
            passages,
            (((1,), (1,)), ((), ())),
            preferred_element_type=jnp.float32,
        )
        * score_scale
    )
    local_peak = jnp.max(scores, axis=1)
    local_total = jnp.sum(jnp.exp(scores - local_peak[:, None]), axis=1)

    def combine(former, latter):
        highest = jnp.maximum(former[0], latter[0])
        return (
            highest,
            former[1] * jnp.exp(former[0] - highest) + latter[1] * jnp.exp(latter[0] - highest),
        )

    global_peak, global_total = merged((local_peak, local_total), ("corpus", "tensor"), combine)
    return (scores, global_peak + jnp.log(global_total))


def solution(mesh):
    in_specs = (
        P("corpus", "tensor"),
        P("corpus", "tensor"),
        P("corpus", "tensor"),
        P("corpus", None),
        P("tensor", None),
        P(),
        P(("corpus", "tensor"), None),
        P("corpus"),
    )
    out_specs = (P(None, ("corpus", "tensor")), P())
    return jax.shard_map(
        on_device, mesh=mesh, in_specs=in_specs, out_specs=out_specs, check_vma=False
    )
```

profile of v0, /device:TPU:10, one launch (start us, length us, event | category | flops | bytes accessed | tf_op | source)
XLA Modules:
  0.0 136.0 jit_solution(11040314828113501551)
XLA Ops:
  7.2 0.0 copy-start
  7.2 0.0 copy-start.1
  7.2 0.0 all-reduce.5.cloned.1.call-start
  7.2 0.9 iota_compare_fusion
  8.1 0.7 broadcast_add_fusion
  8.8 0.1 iota_compare_fusion.1
  8.9 1.1 fusion.11
  10.0 0.9 reshape_reshape.6
  10.9 0.1 fusion.9
  11.0 0.2 fusion.17
  11.2 0.9 reshape_reshape.7
  12.1 0.3 convolution_convert_fusion
  12.4 8.7 %fusion.19 = f32[4,4096]{1,0:T(4,128)} fusion(bf16[4,2048]{1,0:T(4,128)(2,1)S(1)} %convert_element_type.39, bf16[2048,4096]{1,0:T(8,128)(2,1)} %param.14), kind=kOutput, calls=%fused_computation.35 | convolution fusion | flops 67108864 | bytes 16859136 | tf_op jit(solution)/shard_map/dot_general | solution.py:58
  21.1 0.0 all-reduce.5.cloned.1.call-update
  21.1 0.3 fusion.10
  21.4 19.0 %all-reduce.5.cloned.1.call-done = f32[4,4096]{1,0:T(4,128)} async-done(((f32[4,4096]{1,0:T(4,128)}), f32[4,4096]{1,0:T(4,128)}) %all-reduce.5.cloned.1.call-update) | async-done | bytes 65552 | tf_op jit(solution)/shard_map/psum | solution.py:59
  40.4 1.0 multiply_reduce_fusion
  41.4 0.9 fusion.14
  42.4 32.8 %all-gather.2 = bf16[16,4,4096]{2,1,0:T(4,128)(2,1)S(1)} all-gather(bf16[1,4,4096]{2,1,0:T(4,128)(2,1)S(1)} %fusion.14), channel_id=1, replica_groups=mesh['corpus'=16,'tensor'=2] {'corpus'}, dimensions={0}, use_global_device_ids=true | all-gather | bytes 557056 | tf_op jit(solution)/shard_map/all_gather | solution.py:63
  75.1 0.1 reshape.76
  75.3 0.9 fusion.18
  76.1 0.0 copy-start.2
  76.1 0.2 exponential_reduce_fusion
  76.3 0.3 dynamic-update-slice
  76.6 0.3 dynamic-update-slice.1
  76.9 50.2 %all-reduce.2 = (f32[2048]{0:T(1024)S(1)}, f32[2048]{0:T(1024)S(1)}) all-reduce(f32[2048]{0:T(1024)S(1)} %dynamic-update-slice, f32[2048]{0:T(1024)S(1)} %dynamic-update-slice.1), channel_id=2, replica_groups=mesh['corpus'=16,'tensor'=2] {'corpus','tensor'}, use_global_device_ids=true, to_apply=%add | all-reduce | flops 4096 | bytes 32768
  127.1 0.1 slice.22
  127.1 0.1 slice.23
  127.2 0.1 reshape.69
  127.3 0.1 reshape.70
  127.4 1.3 while.12
  128.7 0.5 log_add_fusion
  (43 shorter events, 1.0 us)
Async XLA Ops:
  7.2 68.1 %copy-start = (bf16[256,4096]{1,0:T(8,128)(2,1)S(1)}, bf16[256,4096]{1,0:T(8,128)(2,1)}, u32[]{:S(2)}) copy-start(bf16[256,4096]{1,0:T(8,128)(2,1)} %param.16) | copy-start | bytes 6291460
  7.2 13.9 %copy-start.1 = (bf16[64,4096]{1,0:T(8,128)(2,1)S(1)}, bf16[64,4096]{1,0:T(8,128)(2,1)}, u32[]{:S(2)}) copy-start(bf16[64,4096]{1,0:T(8,128)(2,1)} %param.13) | copy-start | bytes 1572868
  7.2 33.3 %copy-start.3 = (f32[4096]{0:T(1024)S(1)}, f32[4096]{0:T(1024)}, u32[]{:S(2)}) copy-start(f32[4096]{0:T(1024)} %param.15) | copy-start | bytes 49156
  7.2 33.2 %all-reduce.5.cloned.1.call-start = ((), (), s32[]{:S(2)}) async-start(), calls=%async_computation | async-start | bytes 131072 | tf_op jit(solution)/shard_map/psum | solution.py:59
  76.1 53.1 %copy-start.2 = (f32[64,256]{1,0:T(8,128)}, f32[64,256]{1,0:T(8,128)S(1)}, u32[]{:S(2)}) copy-start(f32[64,256]{1,0:T(8,128)S(1)} %get-tuple-element.47) | copy-start | bytes 196612
Sparse Core Ops, SparseCore 0:
  21.2 19.1 all-reduce.4
where the time goes:
time: 136 us
  blocking collectives  82.9 us (61%)
  waiting for transfers between devices  19 us (14%)
  between operations  14.1 us (10%)
  matrix products  9.98 us (7%)
  other arithmetic  6.78 us (5%)
  local copies, waits for them, and re-layouts  2.73 us (2%)
    unnamed x1, blocking collectives  50.2 us
    all_gather x1, blocking collectives, on_device(): lax.all_gather(embed, 'corpus', axis=0, tiled=True)  32.8 us
    psum x1, waiting for transfers between devices, on_device(): pooled = last_residual + lax.psum(partial_value, 'tensor')  19 us
    dot_general x1, matrix products, on_device(): jnp.dot(context, out_weight, preferred_element_type=jnp.float32)  8.68 us
  transfers between devices with their start and end apart: 1, of which 1 were waited for; matrix products, arithmetic and copies ran while one was open for 0% of the time, Pallas kernels for 0%

commit v1 on v0

--- a/solution.py
+++ b/solution.py
@@ -56,7 +56,7 @@
     )
     context = attend_last(last_query, key_rows, value_rows, lengths)
     partial_value = jnp.dot(context, out_weight, preferred_element_type=jnp.float32)
-    pooled = last_residual + lax.psum(partial_value, "tensor")
+    pooled = last_residual + jnp.sum(lax.all_gather(partial_value, "tensor"), axis=0)
     embed = normalize_rows(pooled, final_gain)
     scores = (
         lax.dot_general(

time: 136 us -> 104 us (0.76)
  waiting for transfers between devices: 19 us -> 0 us
  between operations: 14.1 us -> 0.76 us
  blocking collectives: 82.9 us -> 85 us
  other arithmetic: 6.78 us -> 5.15 us
    psum x1 -> x0, waiting for transfers between devices: 19 us -> none  [on_device(): pooled = last_residual + lax.psum(partial_value, 'tensor')]
    all_gather x0 -> x1, blocking collectives: none -> 1.9 us  [on_device(): lax.all_gather(partial_value, 'tensor')]
  transfers between devices with their start and end apart: 1 -> 0, of which waited for: 1 -> 0; matrix products, arithmetic and copies ran while one was open for 0% -> 0% of each run, Pallas kernels for 0% -> 0%
where the time goes in v1:
time: 104 us; the launch traced here: 103 us
  blocking collectives  85 us (82%)
  matrix products  9.35 us (9%)
  other arithmetic  5.15 us (5%)
  local copies, waits for them, and re-layouts  2.74 us (3%)
    unnamed x1, blocking collectives  49.6 us
    all_gather x1, blocking collectives, on_device(): lax.all_gather(embed, 'corpus', axis=0, tiled=True)  33.5 us
    dot_general x1, matrix products, on_device(): jnp.dot(context, out_weight, preferred_element_type=jnp.float32)  8.04 us

profile of v1, /device:TPU:10, one launch (start us, length us, event | category | flops | bytes accessed | tf_op | source)
XLA Modules:
  0.0 103.4 jit_solution(16801535027035805018)
XLA Ops:
  0.6 0.0 copy-start
  0.6 0.0 copy-start.1
  0.7 0.0 copy-start.3
  0.7 0.9 iota_compare_fusion
  1.5 0.7 broadcast_add_fusion
  2.2 0.1 iota_compare_fusion.1
  2.3 1.1 %fusion.11 = bf16[4,2048]{1,0:T(4,128)(2,1)S(1)} fusion(pred[4,16]{1,0:T(4,128)(4,1)S(1)} %iota_compare_fusion.1, bf16[64,2048]{1,0:T(8,128)(2,1)} %param.10), kind=kLoop, calls=%fused_computation.19 | loop fusion | flops 385024 | bytes 278592 | tf_op jit(solution)/shard_map/reduce_sum | solution.py:51
  3.4 0.9 reshape_reshape.6
  4.3 0.1 fusion.9
  4.5 0.2 fusion.17
  4.7 0.9 reshape_reshape.7
  5.5 0.3 convolution_convert_fusion
  5.8 8.0 %convolution_bitcast_fusion = f32[1,4,4096]{2,1,0:T(4,128)S(1)} fusion(bf16[4,2048]{1,0:T(4,128)(2,1)S(1)} %convert_element_type.39, bf16[2048,4096]{1,0:T(8,128)(2,1)} %param.14), kind=kOutput, calls=%fused_computation.8 | convolution fusion | flops 67108864 | bytes 16859136 | tf_op jit(solution)/shard_map/dot_general | solution.py:58
  13.9 1.9 %all-gather.3 = f32[2,4,4096]{2,1,0:T(4,128)S(1)} all-gather(f32[1,4,4096]{2,1,0:T(4,128)S(1)} %convolution_bitcast_fusion), channel_id=2, replica_groups=mesh['corpus'=16,'tensor'=2] {'tensor'}, dimensions={0}, use_global_device_ids=true | all-gather | bytes 196608 | tf_op jit(solution)/shard_map/all_gather | solution.py:59
  15.8 0.0 copy-done.1
  15.8 0.3 fusion.10
  16.1 0.2 multiply_reduce_fusion
  16.3 0.1 fusion.14
  16.4 33.5 %all-gather.4 = bf16[16,4,4096]{2,1,0:T(4,128)(2,1)S(1)} all-gather(bf16[1,4,4096]{2,1,0:T(4,128)(2,1)S(1)} %fusion.14), channel_id=1, replica_groups=mesh['corpus'=16,'tensor'=2] {'corpus'}, dimensions={0}, use_global_device_ids=true | all-gather | bytes 557056 | tf_op jit(solution)/shard_map/all_gather | solution.py:63
  49.9 0.1 reshape.79
  50.0 0.9 fusion.18
  50.9 0.0 copy-start.2
  50.9 0.2 exponential_reduce_fusion
  51.1 0.3 dynamic-update-slice.1
  51.4 0.3 dynamic-update-slice
  51.6 49.6 %all-reduce.2 = (f32[2048]{0:T(1024)S(1)}, f32[2048]{0:T(1024)S(1)}) all-reduce(f32[2048]{0:T(1024)S(1)} %dynamic-update-slice, f32[2048]{0:T(1024)S(1)} %dynamic-update-slice.1), channel_id=3, replica_groups=mesh['corpus'=16,'tensor'=2] {'corpus','tensor'}, use_global_device_ids=true, to_apply=%add | all-reduce | flops 4096 | bytes 32768
  101.3 0.1 slice.22
  101.3 0.1 reshape.70
  101.4 0.1 slice.23
  101.5 0.1 reshape.71
  101.6 1.3 %while.12 = (s32[]{:T(128)}, f32[64]{0:T(128)S(1)}, f32[64]{0:T(128)S(1)}, f32[31,64]{1,0:T(8,128)S(1)}, f32[31,64]{1,0:T(8,128)S(1)}, /*index=5*/s32[]{:T(128)}) while((s32[]{:T(128)}, f32[64]{0:T(128)S(1)}, f32[64]{0:T(128)S(1)}, f32[31,64]{1,0:T(8,128)S(1)}, f32[31,64]{1,0:T(8,128)S(1)}, /*index=5*/s32[]{:T(128)}) %tuple.26), condition=%wide.region_9.10_spmd, body=%wide.region_8.9_spmd.sunk | while | flops 386 | bytes 1609 | solution.py:16
  102.9 0.5 log_add_fusion
  (42 shorter events, 1.0 us)
Async XLA Ops:
  0.6 49.4 %copy-start = (bf16[256,4096]{1,0:T(8,128)(2,1)S(1)}, bf16[256,4096]{1,0:T(8,128)(2,1)}, u32[]{:S(2)}) copy-start(bf16[256,4096]{1,0:T(8,128)(2,1)} %param.16) | copy-start | bytes 6291460
  0.6 15.2 %copy-start.1 = (bf16[64,4096]{1,0:T(8,128)(2,1)S(1)}, bf16[64,4096]{1,0:T(8,128)(2,1)}, u32[]{:S(2)}) copy-start(bf16[64,4096]{1,0:T(8,128)(2,1)} %param.13) | copy-start | bytes 1572868
  0.7 15.5 %copy-start.3 = (f32[4096]{0:T(1024)S(1)}, f32[4096]{0:T(1024)}, u32[]{:S(2)}) copy-start(f32[4096]{0:T(1024)} %param.15) | copy-start | bytes 49156
  50.9 52.5 %copy-start.2 = (f32[64,256]{1,0:T(8,128)}, f32[64,256]{1,0:T(8,128)S(1)}, u32[]{:S(2)}) copy-start(f32[64,256]{1,0:T(8,128)S(1)} %get-tuple-element.47) | copy-start | bytes 196612
